TPU v7x, 32 devices: a whole 2x2x4 slice. The times are simulated.
32 devices in a mesh: row: 8 (over y, x, core), col: 4 (over z).
Axes of the slice: x: 2, y: 2, z: 4, core: 2. Of those that a mesh axis runs over, the one named last changes fastest.
Arguments:
- tile_u: float32 [8, 16, 2048, 128], P('row', 'col'), may hold values from -6 to 6
- tile_v: float32 [8, 16, 2048, 128], P('row', 'col'), may hold values from -1.5 to 1.5
- row_panel_u: float32 [8, 2048, 128], P('row', 'col'), may hold values from -6 to 6
- row_panel_v: float32 [8, 2048, 128], P('row', 'col'), may hold values from -0.125 to 0.125
- col_panel_u: float32 [16, 2048, 128], P('row', 'col'), may hold values from -6 to 6
- col_panel_v: float32 [16, 2048, 128], P('row', 'col'), may hold values from -0.125 to 0.125
- diag_inverse: float32 [2048, 2048], P('col'), may hold values from -0.15 to 2, as said below
- sketch: float32 [2048, 128], replicated, may hold values from -0.125 to 0.125
Outputs:
- new_u: float32 [8, 16, 2048, 128], P('row', 'col')
- new_v: float32 [8, 16, 2048, 128], P('row', 'col')
Inputs may be any that keep to these rules, and one draw needn't show every extreme that they name: `diag_inverse`: lower triangular; the diagonal lies between 0.5 and 2, the entries below it between -0.15 and 0.15.
All inputs are finite; a program needn't handle non-finite values.
Results may differ from a plain program's by a relative error of at most 0.0003.
Values sent between devices are 32-bit elements; how exact they have to be, the bound alone decides.
No kernel may reach another device: no remote copies, remote signals or barrier semaphores. Data moves between devices by JAX's collectives and lax.ppermute only.
A program may use at most 128 MiB of HBM per device.

v0:
```python
import math
import jax
import jax.numpy as jnp
from jax import lax
from jax.sharding import PartitionSpec as P

highest = lax.Precision.HIGHEST


def body(tile_u, tile_v, row_panel_u, row_panel_v, col_panel_u, col_panel_v, diag_inverse, sketch):
    first = jnp.einsum(
        "ab,tbk->tak",
        diag_inverse,
        lax.all_gather(row_panel_v, "col", axis=1, tiled=True),
        precision=highest,
    )
    second = jnp.einsum(
        "ab,tbk->tak",
        diag_inverse,
        lax.all_gather(col_panel_v, "col", axis=1, tiled=True),
        precision=highest,
    )
    col_u_rows, col_v_rows = (
        lax.all_gather(col_panel_u, "row", axis=0, tiled=True),
        lax.all_gather(second, "row", axis=0, tiled=True),
    )
    row_u_full = lax.all_gather(row_panel_u, "col", axis=1, tiled=True)
    col_u_full = lax.all_to_all(col_u_rows, "col", split_axis=0, concat_axis=1, tiled=True)
    partial_cores = jnp.einsum("iak,jal->ijkl", first, col_v_rows, precision=highest)
    cores = lax.psum_scatter(partial_cores, "col", scatter_dimension=1, tiled=True)
    branch = -jnp.einsum("iak,ijkl->ijal", row_u_full, cores, precision=highest)
    left_side = jnp.concatenate([tile_u, branch], axis=-1)
    right_side = jnp.concatenate([tile_v, col_u_full[None]], axis=-1)
    projected = jnp.einsum("ijar,ak->ijrk", right_side, sketch, precision=highest)
    sample = jnp.einsum("ijar,ijrk->ijak", left_side, projected, precision=highest)
    gram_matrix = jnp.einsum("ijak,ijal->ijkl", sample, sample, precision=highest)
    factor = jnp.linalg.cholesky(gram_matrix)
    solved_t = jax.scipy.linalg.solve_triangular(factor, jnp.swapaxes(sample, -1, -2), lower=True)
    basis = jnp.swapaxes(solved_t, -1, -2)
    coefficients = jnp.einsum("ijar,ijak->ijrk", left_side, basis, precision=highest)
    scaling = math.sqrt(tile_u.shape[2])
    new_v = jnp.einsum("ijar,ijrk->ijak", right_side, coefficients, precision=highest) / scaling
    return (basis * scaling, new_v)


def solution(mesh):
    in_specs = (
        P("row", "col", None, None),
        P("row", "col", None, None),
        P("row", "col", None),
        P("row", "col", None),
        P("row", "col", None),
        P("row", "col", None),
        P("col", None),
        P(),
    )
    out_specs = (P("row", "col", None, None), P("row", "col", None, None))
    return jax.shard_map(body, mesh=mesh, in_specs=in_specs, out_specs=out_specs, check_vma=False)
```

profile of v0, /device:TPU:0, one launch (start us, length us, event | category | flops | bytes accessed | tf_op | source)
XLA Modules:
  0.0 438.9 jit_solution(14853244521627657069)
XLA Ops:
  7.2 0.0 copy-start
  7.2 0.0 all-gather.6.cloned.1.call-start
  7.2 2.1 copy.31
  9.3 0.0 all-gather.6.cloned.1.call-update
  9.4 0.0 all-gather.14.cloned.1.call-start
  9.4 0.7 all-gather.14.cloned.1.call-update
  10.1 0.0 all-gather.10.cloned.1.call-start
  10.2 0.7 all-gather.10.cloned.1.call-update
  10.9 0.0 all-gather.8.cloned.1.call-start
  10.9 47.6 %all-gather.6.cloned.1.call-done = f32[2,2048,128]{1,2,0:T(8,128)} async-done(((f32[2,512,128]{1,2,0:T(8,128)}), f32[2,2048,128]{1,2,0:T(8,128)}) %all-gather.6.cloned.1.call-update) | async-done | bytes 2097168 | tf_op jit(solution)/shard_map/all_gather | solution.py:20
  58.5 6.2 %fusion.8 = f32[2,512,128]{1,2,0:T(8,128)S(1)} fusion(f32[2,2048,128]{1,2,0:T(8,128)} %all-gather.6.cloned.1.call-done, f32[512,2048]{1,0:T(8,128)} %param.14), kind=kOutput, calls=%fused_computation.14 | convolution fusion | flops 3221225472 | bytes 6815744 | tf_op jit(solution)/shard_map/ab,tbk->tak/dot_general | solution.py:17
  64.8 1.0 copy.32
  65.8 0.0 all-gather.8.cloned.1.call-update
  65.8 30.0 %all-gather.14.cloned.1.call-done = f32[16,512,128]{2,1,0:T(8,128)} async-done(((f32[2,512,128]{2,1,0:T(8,128)}), f32[16,512,128]{2,1,0:T(8,128)}) %all-gather.14.cloned.1.call-update) | async-done | bytes 4194320 | tf_op jit(solution)/shard_map/all_gather | solution.py:24
  95.9 4.8 %all-to-all-start = ((f32[16,512,128]{2,1,0:T(8,128)}), f32[16,512,128]{2,1,0:T(8,128)}, u32[]{:S(2)}, u32[]{:S(2)}) async-start(f32[16,512,128]{2,1,0:T(8,128)} %all-gather.14.cloned.1.call-done), calls=%async_computation.1 | async-start | bytes 8388608 | tf_op jit(solution)/shard_map/all_to_all | solution.py:28
  100.7 0.0 all-gather.12.cloned.1.call-start
  100.8 0.5 all-gather.12.cloned.1.call-update
  101.3 0.2 reduce-scatter.2.cloned.1.call-start
  101.5 52.2 %all-gather.10.cloned.1.call-done = f32[1,2048,128]{2,1,0:T(8,128)} async-done(((f32[1,512,128]{2,1,0:T(8,128)}), f32[1,2048,128]{2,1,0:T(8,128)}) %all-gather.10.cloned.1.call-update) | async-done | bytes 1048592 | tf_op jit(solution)/shard_map/all_gather | solution.py:14
  153.7 7.0 %convolution_bitcast_fusion.1 = f32[512,128,1]{0,1,2:T(8,128)S(1)} fusion(f32[512,2048]{1,0:T(8,128)} %param.14, f32[1,2048,128]{2,1,0:T(8,128)} %all-gather.10.cloned.1.call-done), kind=kOutput, calls=%fused_computation.15 | convolution fusion | flops 1610612736 | bytes 5505024 | tf_op jit(solution)/shard_map/ab,tbk->tak/dot_general | solution.py:11
  160.7 30.1 %all-gather.8.cloned.1.call-done = f32[16,512,128]{2,1,0:T(8,128)} async-done(((f32[2,512,128]{2,1,0:T(8,128)}), f32[16,512,128]{2,1,0:T(8,128)}) %all-gather.8.cloned.1.call-update) | async-done | bytes 4194320 | tf_op jit(solution)/shard_map/all_gather | solution.py:25
  190.7 9.8 %convolution_bitcast_fusion = f32[1,16,128,128]{2,3,1,0:T(8,128)} fusion(f32[16,512,128]{2,1,0:T(8,128)} %all-gather.8.cloned.1.call-done, f32[512,128,1]{0,1,2:T(8,128)S(1)} %convolution_bitcast_fusion.1), kind=kOutput, calls=%fused_computation.13 | convolution fusion | flops 1610612736 | bytes 5505024 | tf_op jit(solution)/shard_map/iak,jal->ijkl/dot_general | solution.py:29
  200.6 0.0 reduce-scatter.2.cloned.1.call-update
  200.6 5.7 %copy.35 = f32[1,4,2048,128]{2,3,1,0:T(8,128)} copy(f32[1,4,2048,128]{3,2,1,0:T(8,128)} %param.8) | data formatting | bytes 8388608 | tf_op args[0]
  206.3 5.4 %copy.37 = f32[1,4,2048,128]{2,3,1,0:T(8,128)} copy(f32[1,4,2048,128]{3,2,1,0:T(8,128)} %param.9) | data formatting | bytes 8388608 | tf_op args[1]
  211.8 16.7 %all-gather.12.cloned.1.call-done = f32[1,2048,128]{2,1,0:T(8,128)} async-done(((f32[1,512,128]{2,1,0:T(8,128)}), f32[1,2048,128]{2,1,0:T(8,128)}) %all-gather.12.cloned.1.call-update) | async-done | bytes 1048592 | tf_op jit(solution)/shard_map/all_gather | solution.py:27
  228.5 28.2 %reduce-scatter.2.cloned.1.call-done = f32[1,4,128,128]{2,3,1,0:T(8,128)} async-done(((f32[1,16,128,128]{2,3,1,0:T(8,128)}), f32[1,4,128,128]{2,3,1,0:T(8,128)}) %reduce-scatter.2.cloned.1.call-update) | async-done | bytes 262160 | tf_op jit(solution)/shard_map/reduce_scatter | solution.py:30
  256.7 6.7 %negate_bitcast_fusion = f32[1,4,2048,128]{2,3,1,0:T(8,128)} fusion(f32[1,2048,128]{2,1,0:T(8,128)} %all-gather.12.cloned.1.call-done, f32[1,4,128,128]{2,3,1,0:T(8,128)} %reduce-scatter.2.cloned.1.call-done), kind=kOutput, calls=%fused_computation.12 | convolution fusion | flops 1611661312 | bytes 5505024 | tf_op jit(solution)/shard_map/iak,ijkl->ijal/dot_general | solution.py:31
  263.4 0.0 all-to-all-done
  263.4 5.4 %copy.36 = f32[4,4,512,128]{2,0,3,1:T(4,128)} copy(f32[4,4,512,128]{3,2,1,0:T(8,128)} %bitcast.15) | data formatting | bytes 8388608 | tf_op jit(solution)/shard_map/all_to_all | solution.py:28
  268.9 6.0 %broadcast_in_dim.9 = f32[1,4,2048,128]{2,3,1,0:T(8,128)} reshape(f32[4,4,512,128]{2,1,3,0:T(4,128)} %bitcast.83) | data formatting | bytes 8388608 | tf_op jit(solution)/shard_map/broadcast_in_dim | solution.py:33
  274.9 0.0 copy-done
  274.9 0.0 copy-start.3
  274.9 0.0 copy-start.5
  274.9 9.7 %fusion.1 = f32[4,256,128]{2,1,0:T(8,128)S(1)} fusion(f32[1,4,2048,128]{2,3,1,0:T(8,128)} %broadcast_in_dim.9, f32[1,4,2048,128]{2,3,1,0:T(8,128)} %copy.37, f32[2048,128]{1,0:T(8,128)S(1)} %copy-done), kind=kOutput, calls=%fused_computation.3 | convolution fusion | flops 3223322624 | bytes 9961472 | tf_op jit(solution)/shard_map/ijar,ak->ijrk/dot_general | solution.py:34
  284.6 0.0 copy-done.3
  284.7 0.0 copy-done.5
  284.7 14.0 %fusion.3 = f32[4,2048,128]{2,1,0:T(8,128)S(1)} fusion(f32[4,256,128]{2,1,0:T(8,128)S(1)} %fusion.1, f32[1,4,2048,128]{2,3,1,0:T(8,128)S(1)} %copy-done.5, f32[1,4,2048,128]{2,3,1,0:T(8,128)S(1)} %copy-done.3), kind=kOutput, calls=%fused_computation.5 | convolution fusion | flops 3223322624 | bytes 13107200 | tf_op jit(solution)/shard_map/ijar,ijrk->ijak/dot_general | solution.py:35
  298.7 0.0 copy-start.2
  298.7 6.9 %fusion.21 = f32[4,128,128]{1,2,0:T(8,128)S(1)} fusion(f32[4,2048,128]{2,1,0:T(8,128)S(1)} %fusion.3), kind=kOutput, calls=%fused_computation.32 | convolution fusion | flops 1610612736 | bytes 4456448 | tf_op jit(solution)/shard_map/ijak,ijal->ijkl/dot_general | solution.py:36
  305.7 0.0 copy-done.2
  305.7 0.1 copy.41
  305.9 47.1 %custom-call.8 = f32[1,4,128,128]{3,2,1,0:T(8,128)S(1)} custom-call(f32[1,4,128,128]{3,2,1,0:T(8,128)S(1)} %fusion.14), custom_call_target="Cholesky" | custom-call | tf_op jit(solution)/shard_map/jit(cholesky)/cholesky | solution.py:37
  353.0 0.1 compare_reduce_fusion
  353.1 0.1 select_bitcast_fusion
  353.3 39.3 %custom-call.9 = f32[4,1,128,128]{2,3,1,0:T(8,128)S(1)} custom-call(f32[4,1,128,128]{3,2,1,0:T(8,128)S(1)} %select_bitcast_fusion), custom_call_target="InvertDiagBlocksLowerTriangular" | custom-call | tf_op jit(solution)/shard_map/jit(_solve_triangular)/vmap()/triangular_solve | solution.py:38
  392.6 0.0 copy-start.4
  392.6 0.0 copy-start.6
  392.6 5.9 %fusion.4 = f32[4,128,2048]{2,1,0:T(8,128)S(1)} fusion(f32[4,2048,128]{2,1,0:T(8,128)} %copy-done.2, f32[4,1,128,128]{2,3,1,0:T(8,128)S(1)} %custom-call.9), kind=kOutput, calls=%fused_computation.6 | convolution fusion | flops 1610612736 | bytes 8650752 | tf_op jit(solution)/shard_map/jit(_solve_triangular)/vmap()/triangular_solve | solution.py:38
  398.5 0.0 copy-done.4
  398.5 0.0 copy-done.6
  398.5 7.4 %fusion.2 = f32[4,256,128]{2,1,0:T(8,128)S(1)} fusion(f32[4,128,2048]{2,1,0:T(8,128)S(1)} %fusion.4, f32[1,4,2048,128]{2,3,1,0:T(8,128)S(1)} %copy-done.6, f32[1,4,2048,128]{2,3,1,0:T(8,128)S(1)} %copy-done.4), kind=kOutput, calls=%fused_computation.4 | convolution fusion | flops 3223322624 | bytes 13107200 | tf_op jit(solution)/shard_map/ijar,ijak->ijrk/dot_general | solution.py:40
  405.9 0.0 copy-start.7
  405.9 0.0 copy-start.8
  405.9 2.5 multiply_bitcast_fusion.1
  408.5 1.1 copy-done.7
  409.6 1.3 copy-done.8
  410.9 0.0 copy-start.1
  410.9 15.5 %multiply_bitcast_fusion = f32[1,4,2048,128]{3,2,1,0:T(8,128)} fusion(f32[4,256,128]{2,1,0:T(8,128)S(1)} %fusion.2, f32[1,4,2048,128]{2,3,1,0:T(8,128)S(1)} %copy-done.8, f32[1,4,2048,128]{2,3,1,0:T(8,128)S(1)} %copy-done.7), kind=kOutput, calls=%fused_computation.10 | convolution fusion | flops 3224371200 | bytes 13107200 | tf_op jit(solution)/shard_map/ijar,ijrk->ijak/dot_general | solution.py:42
  426.4 5.3 %copy.45 = f32[1,4,2048,128]{3,2,1,0:T(8,128)} copy(f32[1,4,2048,128]{2,3,1,0:T(8,128)} %multiply_bitcast_fusion.1) | data formatting | bytes 8388608
  431.7 0.0 copy-done.1
  (4 shorter events, 0.1 us)
Async XLA Ops:
  7.2 267.7 %copy-start = (f32[2048,128]{1,0:T(8,128)S(1)}, f32[2048,128]{1,0:T(8,128)}, u32[]{:S(2)}) copy-start(f32[2048,128]{1,0:T(8,128)} %param.15) | copy-start | bytes 3145732
  7.2 51.4 %all-gather.6.cloned.1.call-start = ((), (), s32[]{:S(2)}) async-start(), calls=%async_computation.2 | async-start | bytes 2621440 | tf_op jit(solution)/shard_map/all_gather | solution.py:20
  9.4 86.5 %all-gather.14.cloned.1.call-start = ((), (), s32[]{:S(2)}) async-start(), calls=%async_computation.7 | async-start | bytes 4718592 | tf_op jit(solution)/shard_map/all_gather | solution.py:24
  10.1 143.6 %all-gather.10.cloned.1.call-start = ((), (), s32[]{:S(2)}) async-start(), calls=%async_computation.4 | async-start | bytes 1310720 | tf_op jit(solution)/shard_map/all_gather | solution.py:14
  10.9 179.9 %all-gather.8.cloned.1.call-start = ((), (), s32[]{:S(2)}) async-start(), calls=%async_computation.3 | async-start | bytes 4718592 | tf_op jit(solution)/shard_map/all_gather | solution.py:25
  95.9 167.6 %all-to-all-start = ((f32[16,512,128]{2,1,0:T(8,128)}), f32[16,512,128]{2,1,0:T(8,128)}, u32[]{:S(2)}, u32[]{:S(2)}) async-start(f32[16,512,128]{2,1,0:T(8,128)} %all-gather.14.cloned.1.call-done), calls=%async_computation.1 | async-start | bytes 8388608 | tf_op jit(solution)/shard_map/all_to_all | solution.py:28
  100.7 127.8 %all-gather.12.cloned.1.call-start = ((), (), s32[]{:S(2)}) async-start(), calls=%async_computation.6 | async-start | bytes 1310720 | tf_op jit(solution)/shard_map/all_gather | solution.py:27
  101.3 155.4 %reduce-scatter.2.cloned.1.call-start = ((), (), s32[]{:S(2)}) async-start(), calls=%async_computation.5 | async-start | bytes 1310720 | tf_op jit(solution)/shard_map/reduce_scatter | solution.py:30
  274.9 9.7 %copy-start.3 = (f32[1,4,2048,128]{2,3,1,0:T(8,128)S(1)}, f32[1,4,2048,128]{2,3,1,0:T(8,128)}, u32[]{:S(2)}) copy-start(f32[1,4,2048,128]{2,3,1,0:T(8,128)} %copy.35) | copy-start | bytes 12582916
  274.9 9.7 %copy-start.5 = (f32[1,4,2048,128]{2,3,1,0:T(8,128)S(1)}, f32[1,4,2048,128]{2,3,1,0:T(8,128)}, u32[]{:S(2)}) copy-start(f32[1,4,2048,128]{2,3,1,0:T(8,128)} %negate_bitcast_fusion) | copy-start | bytes 12582916
  298.7 7.0 %copy-start.2 = (f32[4,2048,128]{2,1,0:T(8,128)}, f32[4,2048,128]{2,1,0:T(8,128)S(1)}, u32[]{:S(2)}) copy-start(f32[4,2048,128]{2,1,0:T(8,128)S(1)} %fusion.3) | copy-start | bytes 12582916
  392.6 5.9 %copy-start.4 = (f32[1,4,2048,128]{2,3,1,0:T(8,128)S(1)}, f32[1,4,2048,128]{2,3,1,0:T(8,128)}, u32[]{:S(2)}) copy-start(f32[1,4,2048,128]{2,3,1,0:T(8,128)} %copy.35) | copy-start | bytes 12582916
  392.6 5.9 %copy-start.6 = (f32[1,4,2048,128]{2,3,1,0:T(8,128)S(1)}, f32[1,4,2048,128]{2,3,1,0:T(8,128)}, u32[]{:S(2)}) copy-start(f32[1,4,2048,128]{2,3,1,0:T(8,128)} %negate_bitcast_fusion) | copy-start | bytes 12582916
  405.9 3.7 copy-start.7
  405.9 5.0 %copy-start.8 = (f32[1,4,2048,128]{2,3,1,0:T(8,128)S(1)}, f32[1,4,2048,128]{2,3,1,0:T(8,128)}, u32[]{:S(2)}) copy-start(f32[1,4,2048,128]{2,3,1,0:T(8,128)} %broadcast_in_dim.9) | copy-start | bytes 12582916
  410.9 20.9 %copy-start.1 = (f32[2048,128]{1,0:T(8,128)S(1)}, f32[2048,128]{1,0:T(8,128)}, u32[]{:S(2)}) copy-start(f32[2048,128]{1,0:T(8,128)} %param.15) | copy-start | bytes 3145732
Sparse Core Ops, SparseCore 0:
  10.1 48.3 all-gather.5
  60.4 35.3 all-gather.13
  97.4 56.2 all-gather.9
  156.0 34.6 all-gather.7
  192.1 36.3 all-gather.11
  231.2 25.4 reduce-scatter.1
where the time goes:
time: 442 us; the launch traced here: 439 us
  waiting for transfers between devices  207 us (47%)
  other arithmetic  89.3 us (20%)
  matrix products  89.2 us (20%)
  local copies, waits for them, and re-layouts  33.7 us (8%)
  between operations  14.6 us (3%)
  starting transfers between devices  5.25 us (1%)
    all_gather x1, waiting for transfers between devices, body(): lax.all_gather(row_panel_v, 'col', axis=1, tiled=True)  52.2 us
    all_gather x1, waiting for transfers between devices, body(): lax.all_gather(col_panel_v, 'col', axis=1, tiled=True)  47.6 us
    another operation x4, other arithmetic, body(): factor = jnp.linalg.cholesky(gram_matrix)  47.3 us
    another operation x3, other arithmetic, body(): jax.scipy.linalg.solve_triangular(factor, jnp.swapaxes(sample, -1, -2), l...  39.4 us
    all_gather x1, waiting for transfers between devices, body(): lax.all_gather(second, 'row', axis=0, tiled=True)  30.1 us
    all_gather x1, waiting for transfers between devices, body(): lax.all_gather(col_panel_u, 'row', axis=0, tiled=True)  30 us
    reduce_scatter x1, waiting for transfers between devices, body(): lax.psum_scatter(partial_cores, 'col', scatter_dimension=1, tiled=True)  28.2 us
    unnamed x22, local copies, waits for them, and re-layouts  21 us
  transfers between devices with their start and end apart: 7, of which 6 were waited for; matrix products, arithmetic and copies ran while one was open for 10% of the time, Pallas kernels for 0%

commit v1 on v0

--- a/solution.py
+++ b/solution.py
@@ -14,11 +14,45 @@
         lax.all_gather(row_panel_v, "col", axis=1, tiled=True),
         precision=highest,
     )
-    second = jnp.einsum(
-        "ab,tbk->tak",
-        diag_inverse,
-        lax.all_gather(col_panel_v, "col", axis=1, tiled=True),
-        precision=highest,
+
+    def start_the_record(obj, axis_key, z_in):
+        t1, part_now, big = (
+            jax.lax.axis_size(axis_key),
+            jax.lax.axis_index(axis_key),
+            obj.shape[1],
+        )
+        i = 0
+        chunks = []
+        while i < t1:
+            chunks.append((i, (i + 1) % t1))
+            i = i + 1
+        steps_seen = []
+        i = 0
+        while i < t1:
+            steps_seen.append((i, (i - 1) % t1))
+            i = i + 1
+        field_out = taken_in = obj
+        t_next = z_in(obj, part_now * big)
+        extra = t1 // 2
+        hop_no = 1
+        while hop_no < extra + 1:
+            field_out = jax.lax.ppermute(field_out, axis_key, chunks)
+            if hop_no < t1 - extra:
+                taken_in = jax.lax.ppermute(taken_in, axis_key, steps_seen)
+                t_next = t_next + z_in(taken_in, (part_now + hop_no) % t1 * big)
+            t_next = t_next + z_in(field_out, (part_now - hop_no) % t1 * big)
+            hop_no = hop_no + 1
+        return t_next
+
+    second = start_the_record(
+        col_panel_v,
+        "col",
+        z_in=lambda shard, start: jnp.einsum(
+            "ab,tbk->tak",
+            lax.dynamic_slice_in_dim(diag_inverse, start, shard.shape[1], axis=1),
+            shard,
+            precision=highest,
+        ),
     )
     col_u_rows, col_v_rows = (
         lax.all_gather(col_panel_u, "row", axis=0, tiled=True),

time: 442 us -> 396 us (0.90)
  waiting for transfers between devices: 207 us -> 157 us
  starting transfers between devices: 5.25 us -> 10.5 us
    all_gather x1 -> x0, waiting for transfers between devices: 47.6 us -> none  [body(): lax.all_gather(col_panel_v, 'col', axis=1, tiled=True)]
    all_gather x1, waiting for transfers between devices: 30 us -> 0.02 us  [body(): lax.all_gather(col_panel_u, 'row', axis=0, tiled=True)]
    ppermute x0 -> x3, waiting for transfers between devices: none -> 28.8 us  [the longest x2 18.8 us: start_the_record(): field_out = jax.lax.ppermute(field_out, axis_key, chunks)]
    ppermute x0 -> x3, starting transfers between devices: none -> 5.2 us  [the longest x2 3.11 us: start_the_record(): field_out = jax.lax.ppermute(field_out, axis_key, chunks)]
    unnamed x22 -> x23, local copies, waits for them, and re-layouts: 21 us -> 19.2 us
  transfers between devices with their start and end apart: 7 -> 9, of which waited for: 6 -> 7; matrix products, arithmetic and copies ran while one was open for 10% -> 11% of each run, Pallas kernels for 0% -> 0%
where the time goes in v1:
time: 396 us; the launch traced here: 392 us
  waiting for transfers between devices  157 us (40%)
  matrix products  90.4 us (23%)
  other arithmetic  89.3 us (23%)
  local copies, waits for them, and re-layouts  30.8 us (8%)
  between operations  14.2 us (4%)
  starting transfers between devices  10.5 us (3%)
    all_gather x1, waiting for transfers between devices, body(): lax.all_gather(row_panel_v, 'col', axis=1, tiled=True)  51 us
    another operation x4, other arithmetic, body(): factor = jnp.linalg.cholesky(gram_matrix)  47.3 us
    another operation x3, other arithmetic, body(): jax.scipy.linalg.solve_triangular(factor, jnp.swapaxes(sample, -1, -2), l...  39.4 us
    all_gather x1, waiting for transfers between devices, body(): lax.all_gather(second, 'row', axis=0, tiled=True)  29.4 us
    reduce_scatter x1, waiting for transfers between devices, body(): lax.psum_scatter(partial_cores, 'col', scatter_dimension=1, tiled=True)  28.7 us
    unnamed x23, local copies, waits for them, and re-layouts  19.2 us
    ppermute x2, waiting for transfers between devices, start_the_record(): field_out = jax.lax.ppermute(field_out, axis_key, chunks)  18.8 us
    all_gather x1, waiting for transfers between devices, body(): row_u_full = lax.all_gather(row_panel_u, 'col', axis=1, tiled=True)  16.7 us
  transfers between devices with their start and end apart: 9, of which 7 were waited for; matrix products, arithmetic and copies ran while one was open for 11% of the time, Pallas kernels for 0%

profile of v1, /device:TPU:0, one launch (start us, length us, event | category | flops | bytes accessed | tf_op | source)
XLA Modules:
  0.0 391.8 jit_solution(15450349545018930019)
XLA Ops:
  7.2 0.0 copy-start
  7.2 0.0 all-gather.11.cloned.1.call-start
  7.2 0.7 all-gather.11.cloned.1.call-update
  7.9 0.0 all-gather.7.cloned.1.call-start
  8.0 0.7 all-gather.7.cloned.1.call-update
  8.7 0.0 all-gather.5.cloned.1.call-start
  8.7 3.1 collective-permute-start.1
  11.8 2.1 collective-permute-start
  13.9 0.0 copy-start.9
  13.9 2.5 fusion.13
  16.4 10.5 %collective-permute-done.1 = f32[2,512,128]{2,1,0:T(8,128)S(1)} collective-permute-done((f32[2,512,128]{2,1,0:T(8,128)}, f32[2,512,128]{2,1,0:T(8,128)S(1)}, u32[]{:S(2)}, u32[]{:S(2)}) %collective-permute-start.1) | collective-permute-done | bytes 524320 | tf_op jit(solution)/shard_map/ppermute | solution.py:39
  26.9 0.0 collective-permute-start.2
  26.9 10.0 %collective-permute-done = f32[2,512,128]{2,1,0:T(8,128)S(1)} collective-permute-done((f32[2,512,128]{2,1,0:T(8,128)}, f32[2,512,128]{2,1,0:T(8,128)S(1)}, u32[]{:S(2)}, u32[]{:S(2)}) %collective-permute-start) | collective-permute-done | bytes 524320 | tf_op jit(solution)/shard_map/ppermute | solution.py:41
  36.9 2.2 convolution_add_fusion.2
  39.1 0.0 copy-done.9
  39.1 1.0 convolution_add_fusion.1
  40.1 8.4 %collective-permute-done.2 = f32[2,512,128]{2,1,0:T(8,128)S(1)} collective-permute-done((f32[2,512,128]{2,1,0:T(8,128)S(1)}, f32[2,512,128]{2,1,0:T(8,128)S(1)}, u32[]{:S(2)}, u32[]{:S(2)}) %collective-permute-start.2) | collective-permute-done | bytes 524320 | tf_op jit(solution)/shard_map/ppermute | solution.py:39
  48.5 1.8 fusion.6
  50.3 0.0 all-gather.5.cloned.1.call-update
  50.3 0.0 all-gather.11.cloned.1.call-done
  50.3 4.9 %all-to-all-start = ((f32[16,512,128]{2,1,0:T(8,128)}), f32[16,512,128]{2,1,0:T(8,128)}, u32[]{:S(2)}, u32[]{:S(2)}) async-start(f32[16,512,128]{2,1,0:T(8,128)} %all-gather.11.cloned.1.call-done), calls=%async_computation.1 | async-start | bytes 8388608 | tf_op jit(solution)/shard_map/all_to_all | solution.py:62
  55.2 0.0 all-gather.9.cloned.1.call-start
  55.2 0.5 all-gather.9.cloned.1.call-update
  55.8 0.3 reduce-scatter.2.cloned.1.call-start
  56.1 51.0 %all-gather.7.cloned.1.call-done = f32[1,2048,128]{2,1,0:T(8,128)} async-done(((f32[1,512,128]{2,1,0:T(8,128)}), f32[1,2048,128]{2,1,0:T(8,128)}) %all-gather.7.cloned.1.call-update) | async-done | bytes 1048592 | tf_op jit(solution)/shard_map/all_gather | solution.py:14
  107.1 7.0 %convolution_bitcast_fusion.1 = f32[512,128,1]{0,1,2:T(8,128)S(1)} fusion(f32[512,2048]{1,0:T(8,128)} %param.14, f32[1,2048,128]{2,1,0:T(8,128)} %all-gather.7.cloned.1.call-done), kind=kOutput, calls=%fused_computation.16 | convolution fusion | flops 1610612736 | bytes 5505024 | tf_op jit(solution)/shard_map/ab,tbk->tak/dot_general | solution.py:11
  114.0 29.4 %all-gather.5.cloned.1.call-done = f32[16,512,128]{2,1,0:T(8,128)} async-done(((f32[2,512,128]{2,1,0:T(8,128)}), f32[16,512,128]{2,1,0:T(8,128)}) %all-gather.5.cloned.1.call-update) | async-done | bytes 4194320 | tf_op jit(solution)/shard_map/all_gather | solution.py:59
  143.4 9.8 %convolution_bitcast_fusion = f32[1,16,128,128]{2,3,1,0:T(8,128)} fusion(f32[16,512,128]{2,1,0:T(8,128)} %all-gather.5.cloned.1.call-done, f32[512,128,1]{0,1,2:T(8,128)S(1)} %convolution_bitcast_fusion.1), kind=kOutput, calls=%fused_computation.11 | convolution fusion | flops 1610612736 | bytes 5505024 | tf_op jit(solution)/shard_map/iak,jal->ijkl/dot_general | solution.py:63
  153.2 0.0 reduce-scatter.2.cloned.1.call-update
  153.2 5.9 %copy.33 = f32[1,4,2048,128]{2,3,1,0:T(8,128)} copy(f32[1,4,2048,128]{3,2,1,0:T(8,128)} %param.8) | data formatting | bytes 8388608 | tf_op args[0]
  159.2 5.5 %copy.35 = f32[1,4,2048,128]{2,3,1,0:T(8,128)} copy(f32[1,4,2048,128]{3,2,1,0:T(8,128)} %param.9) | data formatting | bytes 8388608 | tf_op args[1]
  164.7 16.7 %all-gather.9.cloned.1.call-done = f32[1,2048,128]{2,1,0:T(8,128)} async-done(((f32[1,512,128]{2,1,0:T(8,128)}), f32[1,2048,128]{2,1,0:T(8,128)}) %all-gather.9.cloned.1.call-update) | async-done | bytes 1048592 | tf_op jit(solution)/shard_map/all_gather | solution.py:61
  181.4 28.7 %reduce-scatter.2.cloned.1.call-done = f32[1,4,128,128]{2,3,1,0:T(8,128)} async-done(((f32[1,16,128,128]{2,3,1,0:T(8,128)}), f32[1,4,128,128]{2,3,1,0:T(8,128)}) %reduce-scatter.2.cloned.1.call-update) | async-done | bytes 262160 | tf_op jit(solution)/shard_map/reduce_scatter | solution.py:64
  210.1 6.7 %negate_bitcast_fusion = f32[1,4,2048,128]{2,3,1,0:T(8,128)} fusion(f32[1,2048,128]{2,1,0:T(8,128)} %all-gather.9.cloned.1.call-done, f32[1,4,128,128]{2,3,1,0:T(8,128)} %reduce-scatter.2.cloned.1.call-done), kind=kOutput, calls=%fused_computation.10 | convolution fusion | flops 1611661312 | bytes 5505024 | tf_op jit(solution)/shard_map/iak,ijkl->ijal/dot_general | solution.py:65
  216.8 0.0 all-to-all-done
  216.8 5.4 %copy.34 = f32[4,4,512,128]{2,0,3,1:T(4,128)} copy(f32[4,4,512,128]{3,2,1,0:T(8,128)} %bitcast.18) | data formatting | bytes 8388608 | tf_op jit(solution)/shard_map/all_to_all | solution.py:62
  222.2 6.0 %broadcast_in_dim.9 = f32[1,4,2048,128]{2,3,1,0:T(8,128)} reshape(f32[4,4,512,128]{2,1,3,0:T(4,128)} %bitcast.93) | data formatting | bytes 8388608 | tf_op jit(solution)/shard_map/broadcast_in_dim | solution.py:67
  228.3 0.0 copy-done
  228.3 9.5 %fusion.1 = f32[4,256,128]{2,1,0:T(8,128)S(1)} fusion(f32[1,4,2048,128]{2,3,1,0:T(8,128)} %broadcast_in_dim.9, f32[1,4,2048,128]{2,3,1,0:T(8,128)} %copy.35, f32[2048,128]{1,0:T(8,128)S(1)} %copy-done), kind=kOutput, calls=%fused_computation.3 | convolution fusion | flops 3223322624 | bytes 9961472 | tf_op jit(solution)/shard_map/ijar,ak->ijrk/dot_general | solution.py:68
  237.8 0.0 copy-done.3
  237.8 0.0 copy-done.5
  237.8 14.1 %fusion.3 = f32[4,2048,128]{2,1,0:T(8,128)S(1)} fusion(f32[4,256,128]{2,1,0:T(8,128)S(1)} %fusion.1, f32[1,4,2048,128]{2,3,1,0:T(8,128)S(1)} %copy-done.5, f32[1,4,2048,128]{2,3,1,0:T(8,128)S(1)} %copy-done.3), kind=kOutput, calls=%fused_computation.5 | convolution fusion | flops 3223322624 | bytes 13107200 | tf_op jit(solution)/shard_map/ijar,ijrk->ijak/dot_general | solution.py:69
  251.9 0.0 copy-start.2
  251.9 6.9 %fusion.30 = f32[4,128,128]{1,2,0:T(8,128)S(1)} fusion(f32[4,2048,128]{2,1,0:T(8,128)S(1)} %fusion.3), kind=kOutput, calls=%fused_computation.46 | convolution fusion | flops 1610612736 | bytes 4456448 | tf_op jit(solution)/shard_map/ijak,ijal->ijkl/dot_general | solution.py:70
  258.8 0.0 copy-done.2
  258.9 0.1 copy.39
  259.0 47.1 %custom-call.8 = f32[1,4,128,128]{3,2,1,0:T(8,128)S(1)} custom-call(f32[1,4,128,128]{3,2,1,0:T(8,128)S(1)} %fusion.19), custom_call_target="Cholesky" | custom-call | tf_op jit(solution)/shard_map/jit(cholesky)/cholesky | solution.py:71
  306.2 0.1 compare_reduce_fusion
  306.3 0.1 select_bitcast_fusion
  306.5 39.3 %custom-call.9 = f32[4,1,128,128]{2,3,1,0:T(8,128)S(1)} custom-call(f32[4,1,128,128]{3,2,1,0:T(8,128)S(1)} %select_bitcast_fusion), custom_call_target="InvertDiagBlocksLowerTriangular" | custom-call | tf_op jit(solution)/shard_map/jit(_solve_triangular)/vmap()/triangular_solve | solution.py:72
  345.8 0.0 copy-start.4
  345.8 0.0 copy-start.6
  345.8 6.1 %fusion.4 = f32[4,128,2048]{2,1,0:T(8,128)S(1)} fusion(f32[4,2048,128]{2,1,0:T(8,128)} %copy-done.2, f32[4,1,128,128]{2,3,1,0:T(8,128)S(1)} %custom-call.9), kind=kOutput, calls=%fused_computation.6 | convolution fusion | flops 1610612736 | bytes 8650752 | tf_op jit(solution)/shard_map/jit(_solve_triangular)/vmap()/triangular_solve | solution.py:72
  351.9 0.0 copy-done.4
  351.9 0.0 copy-done.6
  351.9 7.4 %fusion.2 = f32[4,256,128]{2,1,0:T(8,128)S(1)} fusion(f32[4,128,2048]{2,1,0:T(8,128)S(1)} %fusion.4, f32[1,4,2048,128]{2,3,1,0:T(8,128)S(1)} %copy-done.6, f32[1,4,2048,128]{2,3,1,0:T(8,128)S(1)} %copy-done.4), kind=kOutput, calls=%fused_computation.4 | convolution fusion | flops 3223322624 | bytes 13107200 | tf_op jit(solution)/shard_map/ijar,ijak->ijrk/dot_general | solution.py:74
  359.3 0.0 copy-start.7
  359.3 0.0 copy-start.8
  359.3 2.5 multiply_bitcast_fusion.1
  361.9 1.1 copy-done.7
  363.0 1.3 copy-done.8
  364.3 15.4 %multiply_bitcast_fusion = f32[1,4,2048,128]{3,2,1,0:T(8,128)} fusion(f32[4,256,128]{2,1,0:T(8,128)S(1)} %fusion.2, f32[1,4,2048,128]{2,3,1,0:T(8,128)S(1)} %copy-done.8, f32[1,4,2048,128]{2,3,1,0:T(8,128)S(1)} %copy-done.7), kind=kOutput, calls=%fused_computation.8 | convolution fusion | flops 3224371200 | bytes 13107200 | tf_op jit(solution)/shard_map/ijar,ijrk->ijak/dot_general | solution.py:76
  379.7 5.3 %copy.43 = f32[1,4,2048,128]{3,2,1,0:T(8,128)} copy(f32[1,4,2048,128]{2,3,1,0:T(8,128)} %multiply_bitcast_fusion.1) | data formatting | bytes 8388608
  385.0 0.0 copy-done.1
  (7 shorter events, 0.1 us)
Async XLA Ops:
  7.2 221.1 %copy-start = (f32[2048,128]{1,0:T(8,128)S(1)}, f32[2048,128]{1,0:T(8,128)}, u32[]{:S(2)}) copy-start(f32[2048,128]{1,0:T(8,128)} %param.15) | copy-start | bytes 3145732
  7.2 43.1 %all-gather.11.cloned.1.call-start = ((), (), s32[]{:S(2)}) async-start(), calls=%async_computation.6 | async-start | bytes 4718592 | tf_op jit(solution)/shard_map/all_gather | solution.py:58
  7.9 99.1 %all-gather.7.cloned.1.call-start = ((), (), s32[]{:S(2)}) async-start(), calls=%async_computation.3 | async-start | bytes 1310720 | tf_op jit(solution)/shard_map/all_gather | solution.py:14
  8.7 134.7 %all-gather.5.cloned.1.call-start = ((), (), s32[]{:S(2)}) async-start(), calls=%async_computation.2 | async-start | bytes 4718592 | tf_op jit(solution)/shard_map/all_gather | solution.py:59
  8.7 18.2 %collective-permute-start.1 = (f32[2,512,128]{2,1,0:T(8,128)}, f32[2,512,128]{2,1,0:T(8,128)S(1)}, u32[]{:S(2)}, u32[]{:S(2)}) collective-permute-start(f32[2,512,128]{2,1,0:T(8,128)} %param.13), channel_id=1, source_target_pairs={{0,1},{1,2},{2,3},{3,0},{4,5},{5,6},{6,7},{7,4},{8,9},{9,10},{10,1... | collective-permute-start | bytes 1572872 | tf_op jit(solution)/shard_map/ppermute | solution.py:39
  11.8 25.1 %collective-permute-start = (f32[2,512,128]{2,1,0:T(8,128)}, f32[2,512,128]{2,1,0:T(8,128)S(1)}, u32[]{:S(2)}, u32[]{:S(2)}) collective-permute-start(f32[2,512,128]{2,1,0:T(8,128)} %param.13), channel_id=1, source_target_pairs={{0,3},{1,0},{2,1},{3,2},{4,7},{5,4},{6,5},{7,6},{8,11},{9,8},{10,9... | collective-permute-start | bytes 1572872 | tf_op jit(solution)/shard_map/ppermute | solution.py:41
  13.9 25.2 %copy-start.9 = (f32[512,2048]{1,0:T(8,128)S(1)}, f32[512,2048]{1,0:T(8,128)}, u32[]{:S(2)}) copy-start(f32[512,2048]{1,0:T(8,128)} %param.14) | copy-start | bytes 12582916
  26.9 21.6 %collective-permute-start.2 = (f32[2,512,128]{2,1,0:T(8,128)S(1)}, f32[2,512,128]{2,1,0:T(8,128)S(1)}, u32[]{:S(2)}, u32[]{:S(2)}) collective-permute-start(f32[2,512,128]{2,1,0:T(8,128)S(1)} %collective-permute-done.1), channel_id=1, source_target_pairs={{0,1},{1,2},{2,3},{3,0},{4,5},{5,6},{6,7},{7,4},{8,9},{9,10},{10,1... | collective-permute-start | bytes 1572872 | tf_op jit(solution)/shard_map/ppermute | solution.py:39
  50.3 166.5 %all-to-all-start = ((f32[16,512,128]{2,1,0:T(8,128)}), f32[16,512,128]{2,1,0:T(8,128)}, u32[]{:S(2)}, u32[]{:S(2)}) async-start(f32[16,512,128]{2,1,0:T(8,128)} %all-gather.11.cloned.1.call-done), calls=%async_computation.1 | async-start | bytes 8388608 | tf_op jit(solution)/shard_map/all_to_all | solution.py:62
  55.2 126.2 %all-gather.9.cloned.1.call-start = ((), (), s32[]{:S(2)}) async-start(), calls=%async_computation.5 | async-start | bytes 1310720 | tf_op jit(solution)/shard_map/all_gather | solution.py:61
  55.8 154.3 %reduce-scatter.2.cloned.1.call-start = ((), (), s32[]{:S(2)}) async-start(), calls=%async_computation.4 | async-start | bytes 1310720 | tf_op jit(solution)/shard_map/reduce_scatter | solution.py:64
  228.3 9.5 %copy-start.3 = (f32[1,4,2048,128]{2,3,1,0:T(8,128)S(1)}, f32[1,4,2048,128]{2,3,1,0:T(8,128)}, u32[]{:S(2)}) copy-start(f32[1,4,2048,128]{2,3,1,0:T(8,128)} %copy.33) | copy-start | bytes 12582916
  228.3 9.5 %copy-start.5 = (f32[1,4,2048,128]{2,3,1,0:T(8,128)S(1)}, f32[1,4,2048,128]{2,3,1,0:T(8,128)}, u32[]{:S(2)}) copy-start(f32[1,4,2048,128]{2,3,1,0:T(8,128)} %negate_bitcast_fusion) | copy-start | bytes 12582916
  251.9 7.0 %copy-start.2 = (f32[4,2048,128]{2,1,0:T(8,128)}, f32[4,2048,128]{2,1,0:T(8,128)S(1)}, u32[]{:S(2)}) copy-start(f32[4,2048,128]{2,1,0:T(8,128)S(1)} %fusion.3) | copy-start | bytes 12582916
  345.8 6.1 %copy-start.4 = (f32[1,4,2048,128]{2,3,1,0:T(8,128)S(1)}, f32[1,4,2048,128]{2,3,1,0:T(8,128)}, u32[]{:S(2)}) copy-start(f32[1,4,2048,128]{2,3,1,0:T(8,128)} %copy.33) | copy-start | bytes 12582916
  345.8 6.1 %copy-start.6 = (f32[1,4,2048,128]{2,3,1,0:T(8,128)S(1)}, f32[1,4,2048,128]{2,3,1,0:T(8,128)}, u32[]{:S(2)}) copy-start(f32[1,4,2048,128]{2,3,1,0:T(8,128)} %negate_bitcast_fusion) | copy-start | bytes 12582916
  359.3 3.7 copy-start.7
  359.3 5.0 %copy-start.8 = (f32[1,4,2048,128]{2,3,1,0:T(8,128)S(1)}, f32[1,4,2048,128]{2,3,1,0:T(8,128)}, u32[]{:S(2)}) copy-start(f32[1,4,2048,128]{2,3,1,0:T(8,128)} %broadcast_in_dim.9) | copy-start | bytes 12582916
  364.3 20.7 %copy-start.1 = (f32[2048,128]{1,0:T(8,128)S(1)}, f32[2048,128]{1,0:T(8,128)}, u32[]{:S(2)}) copy-start(f32[2048,128]{1,0:T(8,128)} %param.15) | copy-start | bytes 3145732
Sparse Core Ops, SparseCore 0:
  9.9 39.2 all-gather.10
  50.8 56.2 all-gather.6
  109.5 33.8 all-gather.4
  144.8 36.5 all-gather.8
  184.1 25.9 reduce-scatter.1
